TPU v7x, 16 devices: a whole 2x2x2 slice. The times are simulated.
16 devices in a mesh: ens: 4 (over z, y), sp: 4 (over x, core).
Axes of the slice: x: 2, y: 2, z: 2, core: 2. Of those that a mesh axis runs over, the one named last changes fastest.
Arguments:
- x_seq: bfloat16 [32768, 128], P(('ens', 'sp')), parts along dimension 0
- w_past: bfloat16 [2, 10, 128, 256], replicated
- w_now: bfloat16 [2, 10, 128, 256], replicated
- b_conv: float32 [2, 10, 256], replicated
- w_res: bfloat16 [2, 10, 128, 128], replicated
- w_skip: bfloat16 [2, 10, 128, 128], replicated
- w_out1: bfloat16 [128, 128], replicated
- b_out1: float32 [128], replicated
- w_out2: bfloat16 [128, 256], replicated
- b_out2: float32 [256], replicated
Outputs:
- output 1: float32 [32768, 256], P(('ens', 'sp')), parts along dimension 0
- output 2: bfloat16 [32768, 128], P(('ens', 'sp')), parts along dimension 0
There are 4 independent parts. A program takes and returns all parts, laid end to end along the dimension named above; an argument that names none is the same for every part.
All inputs are finite; a program needn't handle non-finite values.
Results may differ from a plain program's by a relative error of at most 0.0142219.
Values are sent between devices in bfloat16 or wider.
A program may use at most 1 GiB of HBM per device.

v0:
```python
import jax
import jax.numpy as jnp
from jax import lax
from jax.sharding import PartitionSpec as P


def solution(mesh):
    seq_devs = mesh.shape["sp"]
    shift_perm = [(src, src + 1) for src in range(seq_devs - 1)]
    row_spec = P(("ens", "sp"), None)

    def local_stack(x_seq, w_past, w_now, b_conv, w_res, w_skip, w_out1, b_out1, w_out2, b_out2):
        stacks, cycle = w_past.shape[0], w_past.shape[1]
        gate_ch = b_conv.shape[-1] // 2
        hidden = x_seq
        skip_sum = jnp.zeros((x_seq.shape[0], w_skip.shape[-1]), jnp.float32)
        for stack_idx in range(stacks):
            for layer_pos in range(cycle):
                dilation = 2 ** layer_pos
                halo_rows = lax.ppermute(hidden[-dilation:], "sp", perm=shift_perm)
                shifted = jnp.concatenate([halo_rows, hidden[:-dilation]], axis=0)
                pre_act = (jnp.dot(shifted, w_past[stack_idx, layer_pos], preferred_element_type=jnp.float32)
                           + jnp.dot(hidden, w_now[stack_idx, layer_pos], preferred_element_type=jnp.float32)
                           + b_conv[stack_idx, layer_pos])
                gated = (jnp.tanh(pre_act[:, :gate_ch]) * jax.nn.sigmoid(pre_act[:, gate_ch:])).astype(jnp.bfloat16)
                hidden = (hidden.astype(jnp.float32) + jnp.dot(gated, w_res[stack_idx, layer_pos], preferred_element_type=jnp.float32)).astype(jnp.bfloat16)
                skip_sum = skip_sum + jnp.dot(gated, w_skip[stack_idx, layer_pos], preferred_element_type=jnp.float32)
        skip_act = jax.nn.relu(skip_sum).astype(jnp.bfloat16)
        mid_act = jax.nn.relu(jnp.dot(skip_act, w_out1, preferred_element_type=jnp.float32) + b_out1).astype(jnp.bfloat16)
        logits = jnp.dot(mid_act, w_out2, preferred_element_type=jnp.float32) + b_out2
        return (logits, hidden)

    return jax.shard_map(
        local_stack,
        mesh=mesh,
        in_specs=(row_spec, P(), P(), P(), P(), P(), P(), P(), P(), P()),
        out_specs=(row_spec, row_spec),
        check_vma=False,
    )
```

profile of v0, /device:TPU:1, one launch (start us, length us, event | category | flops | bytes accessed | tf_op | source)
XLA Modules:
  0.0 139.8 jit_solution(7221479154996458045)
XLA Ops:
  1.5 4.5 %collective-permute-start = (bf16[1,128]{1,0:T(2,128)(2,1)S(1)}, bf16[1,128]{1,0:T(2,128)(2,1)S(1)}, u32[]{:S(2)}, u32[]{:S(2)}) collective-permute-start(bf16[1,128]{1,0:T(2,128)(2,1)S(1)} %slice.540), channel_id=1, source_target_pairs={{0,1},{1,2},{2,3},{4,5},{5,6},{6,7},{8,9},{9,10},{10,11},{12,13},{... | collective-permute-start | bytes 776 | tf_op jit(solution)/shard_map/ppermute | solution.py:20
  6.0 1.5 %fusion.262 = f32[2048,256]{1,0:T(8,128)S(1)} fusion(bf16[2048,128]{1,0:T(8,128)(2,1)} %param.10, bf16[2,10,128,256]{3,2,1,0:T(8,128)(2,1)} %param.12), kind=kOutput, calls=%fused_computation.363 | convolution fusion | flops 134217728 | bytes 2686976 | tf_op jit(solution)/shard_map/dot_general | solution.py:23
  9.9 3.3 %collective-permute-start.1 = (bf16[2,128]{1,0:T(2,128)(2,1)S(1)}, bf16[2,128]{1,0:T(2,128)(2,1)S(1)}, u32[]{:S(2)}, u32[]{:S(2)}) collective-permute-start(bf16[2,128]{1,0:T(2,128)(2,1)S(1)} %slice.722), channel_id=1, source_target_pairs={{0,1},{1,2},{2,3},{4,5},{5,6},{6,7},{8,9},{9,10},{10,11},{12,13},{... | collective-permute-start | bytes 1544 | tf_op jit(solution)/shard_map/ppermute | solution.py:20
  15.6 4.2 %collective-permute-start.2 = (bf16[4,128]{1,0:T(4,128)(2,1)S(1)}, bf16[4,128]{1,0:T(4,128)(2,1)S(1)}, u32[]{:S(2)}, u32[]{:S(2)}) collective-permute-start(bf16[4,128]{1,0:T(4,128)(2,1)S(1)} %slice.726), channel_id=1, source_target_pairs={{0,1},{1,2},{2,3},{4,5},{5,6},{6,7},{8,9},{9,10},{10,11},{12,13},{... | collective-permute-start | bytes 3080 | tf_op jit(solution)/shard_map/ppermute | solution.py:20
  22.0 4.2 %collective-permute-start.3 = (bf16[8,128]{1,0:T(8,128)(2,1)S(1)}, bf16[8,128]{1,0:T(8,128)(2,1)S(1)}, u32[]{:S(2)}, u32[]{:S(2)}) collective-permute-start(bf16[8,128]{1,0:T(8,128)(2,1)S(1)} %slice.730), channel_id=1, source_target_pairs={{0,1},{1,2},{2,3},{4,5},{5,6},{6,7},{8,9},{9,10},{10,11},{12,13},{... | collective-permute-start | bytes 6152 | tf_op jit(solution)/shard_map/ppermute | solution.py:20
  28.5 4.2 %collective-permute-start.4 = (bf16[16,128]{1,0:T(8,128)(2,1)S(1)}, bf16[16,128]{1,0:T(8,128)(2,1)S(1)}, u32[]{:S(2)}, u32[]{:S(2)}) collective-permute-start(bf16[16,128]{1,0:T(8,128)(2,1)S(1)} %slice.734), channel_id=1, source_target_pairs={{0,1},{1,2},{2,3},{4,5},{5,6},{6,7},{8,9},{9,10},{10,11},{12,13},{... | collective-permute-start | bytes 12296 | tf_op jit(solution)/shard_map/ppermute | solution.py:20
  35.0 4.2 %collective-permute-start.5 = (bf16[32,128]{1,0:T(8,128)(2,1)S(1)}, bf16[32,128]{1,0:T(8,128)(2,1)S(1)}, u32[]{:S(2)}, u32[]{:S(2)}) collective-permute-start(bf16[32,128]{1,0:T(8,128)(2,1)S(1)} %slice.738), channel_id=1, source_target_pairs={{0,1},{1,2},{2,3},{4,5},{5,6},{6,7},{8,9},{9,10},{10,11},{12,13},{... | collective-permute-start | bytes 24584 | tf_op jit(solution)/shard_map/ppermute | solution.py:20
  41.5 4.2 %collective-permute-start.6 = (bf16[64,128]{1,0:T(8,128)(2,1)S(1)}, bf16[64,128]{1,0:T(8,128)(2,1)S(1)}, u32[]{:S(2)}, u32[]{:S(2)}) collective-permute-start(bf16[64,128]{1,0:T(8,128)(2,1)S(1)} %slice.742), channel_id=1, source_target_pairs={{0,1},{1,2},{2,3},{4,5},{5,6},{6,7},{8,9},{9,10},{10,11},{12,13},{... | collective-permute-start | bytes 49160 | tf_op jit(solution)/shard_map/ppermute | solution.py:20
  48.1 4.4 %collective-permute-start.7 = (bf16[128,128]{1,0:T(8,128)(2,1)S(1)}, bf16[128,128]{1,0:T(8,128)(2,1)S(1)}, u32[]{:S(2)}, u32[]{:S(2)}) collective-permute-start(bf16[128,128]{1,0:T(8,128)(2,1)S(1)} %slice.746), channel_id=1, source_target_pairs={{0,1},{1,2},{2,3},{4,5},{5,6},{6,7},{8,9},{9,10},{10,11},{12,13},{... | collective-permute-start | bytes 98312 | tf_op jit(solution)/shard_map/ppermute | solution.py:20
  54.9 4.2 %collective-permute-start.8 = (bf16[256,128]{1,0:T(8,128)(2,1)S(1)}, bf16[256,128]{1,0:T(8,128)(2,1)S(1)}, u32[]{:S(2)}, u32[]{:S(2)}) collective-permute-start(bf16[256,128]{1,0:T(8,128)(2,1)S(1)} %slice.750), channel_id=1, source_target_pairs={{0,1},{1,2},{2,3},{4,5},{5,6},{6,7},{8,9},{9,10},{10,11},{12,13},{... | collective-permute-start | bytes 196616 | tf_op jit(solution)/shard_map/ppermute | solution.py:20
  62.0 4.3 %collective-permute-start.9 = (bf16[512,128]{1,0:T(8,128)(2,1)S(1)}, bf16[512,128]{1,0:T(8,128)(2,1)S(1)}, u32[]{:S(2)}, u32[]{:S(2)}) collective-permute-start(bf16[512,128]{1,0:T(8,128)(2,1)S(1)} %slice.754), channel_id=1, source_target_pairs={{0,1},{1,2},{2,3},{4,5},{5,6},{6,7},{8,9},{9,10},{10,11},{12,13},{... | collective-permute-start | bytes 393224 | tf_op jit(solution)/shard_map/ppermute | solution.py:20
  66.6 1.6 %collective-permute-done.9 = bf16[512,128]{1,0:T(8,128)(2,1)S(1)} collective-permute-done((bf16[512,128]{1,0:T(8,128)(2,1)S(1)}, bf16[512,128]{1,0:T(8,128)(2,1)S(1)}, u32[]{:S(2)}, u32[]{:S(2)}) %collective-permute-start.9) | collective-permute-done | bytes 131104 | tf_op jit(solution)/shard_map/ppermute | solution.py:20
  69.7 4.3 %collective-permute-start.10 = (bf16[1,128]{1,0:T(2,128)(2,1)S(1)}, bf16[1,128]{1,0:T(2,128)(2,1)S(1)}, u32[]{:S(2)}, u32[]{:S(2)}) collective-permute-start(bf16[1,128]{1,0:T(2,128)(2,1)S(1)} %slice.758), channel_id=1, source_target_pairs={{0,1},{1,2},{2,3},{4,5},{5,6},{6,7},{8,9},{9,10},{10,11},{12,13},{... | collective-permute-start | bytes 776 | tf_op jit(solution)/shard_map/ppermute | solution.py:20
  76.4 4.2 %collective-permute-start.11 = (bf16[2,128]{1,0:T(2,128)(2,1)S(1)}, bf16[2,128]{1,0:T(2,128)(2,1)S(1)}, u32[]{:S(2)}, u32[]{:S(2)}) collective-permute-start(bf16[2,128]{1,0:T(2,128)(2,1)S(1)} %slice.762), channel_id=1, source_target_pairs={{0,1},{1,2},{2,3},{4,5},{5,6},{6,7},{8,9},{9,10},{10,11},{12,13},{... | collective-permute-start | bytes 1544 | tf_op jit(solution)/shard_map/ppermute | solution.py:20
  82.9 4.2 %collective-permute-start.12 = (bf16[4,128]{1,0:T(4,128)(2,1)S(1)}, bf16[4,128]{1,0:T(4,128)(2,1)S(1)}, u32[]{:S(2)}, u32[]{:S(2)}) collective-permute-start(bf16[4,128]{1,0:T(4,128)(2,1)S(1)} %slice.766), channel_id=1, source_target_pairs={{0,1},{1,2},{2,3},{4,5},{5,6},{6,7},{8,9},{9,10},{10,11},{12,13},{... | collective-permute-start | bytes 3080 | tf_op jit(solution)/shard_map/ppermute | solution.py:20
  89.4 4.2 %collective-permute-start.13 = (bf16[8,128]{1,0:T(8,128)(2,1)S(1)}, bf16[8,128]{1,0:T(8,128)(2,1)S(1)}, u32[]{:S(2)}, u32[]{:S(2)}) collective-permute-start(bf16[8,128]{1,0:T(8,128)(2,1)S(1)} %slice.770), channel_id=1, source_target_pairs={{0,1},{1,2},{2,3},{4,5},{5,6},{6,7},{8,9},{9,10},{10,11},{12,13},{... | collective-permute-start | bytes 6152 | tf_op jit(solution)/shard_map/ppermute | solution.py:20
  95.8 4.4 %collective-permute-start.14 = (bf16[16,128]{1,0:T(8,128)(2,1)S(1)}, bf16[16,128]{1,0:T(8,128)(2,1)S(1)}, u32[]{:S(2)}, u32[]{:S(2)}) collective-permute-start(bf16[16,128]{1,0:T(8,128)(2,1)S(1)} %slice.774), channel_id=1, source_target_pairs={{0,1},{1,2},{2,3},{4,5},{5,6},{6,7},{8,9},{9,10},{10,11},{12,13},{... | collective-permute-start | bytes 12296 | tf_op jit(solution)/shard_map/ppermute | solution.py:20
  102.3 4.2 %collective-permute-start.15 = (bf16[32,128]{1,0:T(8,128)(2,1)S(1)}, bf16[32,128]{1,0:T(8,128)(2,1)S(1)}, u32[]{:S(2)}, u32[]{:S(2)}) collective-permute-start(bf16[32,128]{1,0:T(8,128)(2,1)S(1)} %slice.778), channel_id=1, source_target_pairs={{0,1},{1,2},{2,3},{4,5},{5,6},{6,7},{8,9},{9,10},{10,11},{12,13},{... | collective-permute-start | bytes 24584 | tf_op jit(solution)/shard_map/ppermute | solution.py:20
  108.8 4.2 %collective-permute-start.16 = (bf16[64,128]{1,0:T(8,128)(2,1)S(1)}, bf16[64,128]{1,0:T(8,128)(2,1)S(1)}, u32[]{:S(2)}, u32[]{:S(2)}) collective-permute-start(bf16[64,128]{1,0:T(8,128)(2,1)S(1)} %slice.782), channel_id=1, source_target_pairs={{0,1},{1,2},{2,3},{4,5},{5,6},{6,7},{8,9},{9,10},{10,11},{12,13},{... | collective-permute-start | bytes 49160 | tf_op jit(solution)/shard_map/ppermute | solution.py:20
  115.4 4.2 %collective-permute-start.17 = (bf16[128,128]{1,0:T(8,128)(2,1)S(1)}, bf16[128,128]{1,0:T(8,128)(2,1)S(1)}, u32[]{:S(2)}, u32[]{:S(2)}) collective-permute-start(bf16[128,128]{1,0:T(8,128)(2,1)S(1)} %slice.786), channel_id=1, source_target_pairs={{0,1},{1,2},{2,3},{4,5},{5,6},{6,7},{8,9},{9,10},{10,11},{12,13},{... | collective-permute-start | bytes 98312 | tf_op jit(solution)/shard_map/ppermute | solution.py:20
  122.2 4.2 %collective-permute-start.18 = (bf16[256,128]{1,0:T(8,128)(2,1)S(1)}, bf16[256,128]{1,0:T(8,128)(2,1)S(1)}, u32[]{:S(2)}, u32[]{:S(2)}) collective-permute-start(bf16[256,128]{1,0:T(8,128)(2,1)S(1)} %slice.790), channel_id=1, source_target_pairs={{0,1},{1,2},{2,3},{4,5},{5,6},{6,7},{8,9},{9,10},{10,11},{12,13},{... | collective-permute-start | bytes 196616 | tf_op jit(solution)/shard_map/ppermute | solution.py:20
  129.3 4.3 %collective-permute-start.19 = (bf16[512,128]{1,0:T(8,128)(2,1)S(1)}, bf16[512,128]{1,0:T(8,128)(2,1)S(1)}, u32[]{:S(2)}, u32[]{:S(2)}) collective-permute-start(bf16[512,128]{1,0:T(8,128)(2,1)S(1)} %slice.794), channel_id=1, source_target_pairs={{0,1},{1,2},{2,3},{4,5},{5,6},{6,7},{8,9},{9,10},{10,11},{12,13},{... | collective-permute-start | bytes 393224 | tf_op jit(solution)/shard_map/ppermute | solution.py:20
  133.9 1.6 %collective-permute-done.19 = bf16[512,128]{1,0:T(8,128)(2,1)S(1)} collective-permute-done((bf16[512,128]{1,0:T(8,128)(2,1)S(1)}, bf16[512,128]{1,0:T(8,128)(2,1)S(1)}, u32[]{:S(2)}, u32[]{:S(2)}) %collective-permute-start.19) | collective-permute-done | bytes 131104 | tf_op jit(solution)/shard_map/ppermute | solution.py:20
  138.0 1.7 %convolution_add_fusion = f32[2048,256]{1,0:T(8,128)} fusion(bf16[2048,128]{1,0:T(8,128)(2,1)S(1)} %fusion.42, bf16[128,256]{1,0:T(8,128)(2,1)S(1)} %copy-done, f32[256]{0:T(256)S(1)} %copy-done.8), kind=kOutput, calls=%fused_computation | convolution fusion | flops 134742016 | bytes 2688000 | tf_op jit(solution)/shard_map/dot_general | solution.py:30
  (173 shorter events, 47.5 us)
Async XLA Ops:
  0.6 137.4 %copy-start = (bf16[128,256]{1,0:T(8,128)(2,1)S(1)}, bf16[128,256]{1,0:T(8,128)(2,1)}, u32[]{:S(2)}) copy-start(bf16[128,256]{1,0:T(8,128)(2,1)} %param.18) | copy-start | bytes 196612
  0.6 6.9 %copy-start.1 = (bf16[2048,128]{1,0:T(8,128)(2,1)S(1)}, bf16[2048,128]{1,0:T(8,128)(2,1)}, u32[]{:S(2)}) copy-start(bf16[2048,128]{1,0:T(8,128)(2,1)} %param.10) | copy-start | bytes 1572868
  0.7 6.8 %copy-start.7 = (f32[2,10,256]{2,0,1:T(2,128)S(1)}, f32[2,10,256]{2,0,1:T(2,128)}, u32[]{:S(2)}) copy-start(f32[2,10,256]{2,0,1:T(2,128)} %param.13) | copy-start | bytes 61444
  0.7 6.9 %copy-start.2 = (bf16[2,10,128,256]{3,2,1,0:T(8,128)(2,1)S(1)}, bf16[2,10,128,256]{3,2,1,0:T(8,128)(2,1)}, u32[]{:S(2)}) copy-start(bf16[2,10,128,256]{3,2,1,0:T(8,128)(2,1)} %param.11) | copy-start | bytes 3932164
  1.5 6.0 %collective-permute-start = (bf16[1,128]{1,0:T(2,128)(2,1)S(1)}, bf16[1,128]{1,0:T(2,128)(2,1)S(1)}, u32[]{:S(2)}, u32[]{:S(2)}) collective-permute-start(bf16[1,128]{1,0:T(2,128)(2,1)S(1)} %slice.540), channel_id=1, source_target_pairs={{0,1},{1,2},{2,3},{4,5},{5,6},{6,7},{8,9},{9,10},{10,11},{12,13},{... | collective-permute-start | bytes 776 | tf_op jit(solution)/shard_map/ppermute | solution.py:20
  9.9 4.1 %collective-permute-start.1 = (bf16[2,128]{1,0:T(2,128)(2,1)S(1)}, bf16[2,128]{1,0:T(2,128)(2,1)S(1)}, u32[]{:S(2)}, u32[]{:S(2)}) collective-permute-start(bf16[2,128]{1,0:T(2,128)(2,1)S(1)} %slice.722), channel_id=1, source_target_pairs={{0,1},{1,2},{2,3},{4,5},{5,6},{6,7},{8,9},{9,10},{10,11},{12,13},{... | collective-permute-start | bytes 1544 | tf_op jit(solution)/shard_map/ppermute | solution.py:20
  15.6 4.9 %collective-permute-start.2 = (bf16[4,128]{1,0:T(4,128)(2,1)S(1)}, bf16[4,128]{1,0:T(4,128)(2,1)S(1)}, u32[]{:S(2)}, u32[]{:S(2)}) collective-permute-start(bf16[4,128]{1,0:T(4,128)(2,1)S(1)} %slice.726), channel_id=1, source_target_pairs={{0,1},{1,2},{2,3},{4,5},{5,6},{6,7},{8,9},{9,10},{10,11},{12,13},{... | collective-permute-start | bytes 3080 | tf_op jit(solution)/shard_map/ppermute | solution.py:20
  22.0 4.9 %collective-permute-start.3 = (bf16[8,128]{1,0:T(8,128)(2,1)S(1)}, bf16[8,128]{1,0:T(8,128)(2,1)S(1)}, u32[]{:S(2)}, u32[]{:S(2)}) collective-permute-start(bf16[8,128]{1,0:T(8,128)(2,1)S(1)} %slice.730), channel_id=1, source_target_pairs={{0,1},{1,2},{2,3},{4,5},{5,6},{6,7},{8,9},{9,10},{10,11},{12,13},{... | collective-permute-start | bytes 6152 | tf_op jit(solution)/shard_map/ppermute | solution.py:20
  28.5 4.9 %collective-permute-start.4 = (bf16[16,128]{1,0:T(8,128)(2,1)S(1)}, bf16[16,128]{1,0:T(8,128)(2,1)S(1)}, u32[]{:S(2)}, u32[]{:S(2)}) collective-permute-start(bf16[16,128]{1,0:T(8,128)(2,1)S(1)} %slice.734), channel_id=1, source_target_pairs={{0,1},{1,2},{2,3},{4,5},{5,6},{6,7},{8,9},{9,10},{10,11},{12,13},{... | collective-permute-start | bytes 12296 | tf_op jit(solution)/shard_map/ppermute | solution.py:20
  35.0 5.0 %collective-permute-start.5 = (bf16[32,128]{1,0:T(8,128)(2,1)S(1)}, bf16[32,128]{1,0:T(8,128)(2,1)S(1)}, u32[]{:S(2)}, u32[]{:S(2)}) collective-permute-start(bf16[32,128]{1,0:T(8,128)(2,1)S(1)} %slice.738), channel_id=1, source_target_pairs={{0,1},{1,2},{2,3},{4,5},{5,6},{6,7},{8,9},{9,10},{10,11},{12,13},{... | collective-permute-start | bytes 24584 | tf_op jit(solution)/shard_map/ppermute | solution.py:20
  41.5 5.1 %collective-permute-start.6 = (bf16[64,128]{1,0:T(8,128)(2,1)S(1)}, bf16[64,128]{1,0:T(8,128)(2,1)S(1)}, u32[]{:S(2)}, u32[]{:S(2)}) collective-permute-start(bf16[64,128]{1,0:T(8,128)(2,1)S(1)} %slice.742), channel_id=1, source_target_pairs={{0,1},{1,2},{2,3},{4,5},{5,6},{6,7},{8,9},{9,10},{10,11},{12,13},{... | collective-permute-start | bytes 49160 | tf_op jit(solution)/shard_map/ppermute | solution.py:20
  48.1 5.2 %collective-permute-start.7 = (bf16[128,128]{1,0:T(8,128)(2,1)S(1)}, bf16[128,128]{1,0:T(8,128)(2,1)S(1)}, u32[]{:S(2)}, u32[]{:S(2)}) collective-permute-start(bf16[128,128]{1,0:T(8,128)(2,1)S(1)} %slice.746), channel_id=1, source_target_pairs={{0,1},{1,2},{2,3},{4,5},{5,6},{6,7},{8,9},{9,10},{10,11},{12,13},{... | collective-permute-start | bytes 98312 | tf_op jit(solution)/shard_map/ppermute | solution.py:20
  54.9 5.5 %collective-permute-start.8 = (bf16[256,128]{1,0:T(8,128)(2,1)S(1)}, bf16[256,128]{1,0:T(8,128)(2,1)S(1)}, u32[]{:S(2)}, u32[]{:S(2)}) collective-permute-start(bf16[256,128]{1,0:T(8,128)(2,1)S(1)} %slice.750), channel_id=1, source_target_pairs={{0,1},{1,2},{2,3},{4,5},{5,6},{6,7},{8,9},{9,10},{10,11},{12,13},{... | collective-permute-start | bytes 196616 | tf_op jit(solution)/shard_map/ppermute | solution.py:20
  62.0 6.2 %collective-permute-start.9 = (bf16[512,128]{1,0:T(8,128)(2,1)S(1)}, bf16[512,128]{1,0:T(8,128)(2,1)S(1)}, u32[]{:S(2)}, u32[]{:S(2)}) collective-permute-start(bf16[512,128]{1,0:T(8,128)(2,1)S(1)} %slice.754), channel_id=1, source_target_pairs={{0,1},{1,2},{2,3},{4,5},{5,6},{6,7},{8,9},{9,10},{10,11},{12,13},{... | collective-permute-start | bytes 393224 | tf_op jit(solution)/shard_map/ppermute | solution.py:20
  69.7 5.1 %collective-permute-start.10 = (bf16[1,128]{1,0:T(2,128)(2,1)S(1)}, bf16[1,128]{1,0:T(2,128)(2,1)S(1)}, u32[]{:S(2)}, u32[]{:S(2)}) collective-permute-start(bf16[1,128]{1,0:T(2,128)(2,1)S(1)} %slice.758), channel_id=1, source_target_pairs={{0,1},{1,2},{2,3},{4,5},{5,6},{6,7},{8,9},{9,10},{10,11},{12,13},{... | collective-permute-start | bytes 776 | tf_op jit(solution)/shard_map/ppermute | solution.py:20
  76.4 4.9 %collective-permute-start.11 = (bf16[2,128]{1,0:T(2,128)(2,1)S(1)}, bf16[2,128]{1,0:T(2,128)(2,1)S(1)}, u32[]{:S(2)}, u32[]{:S(2)}) collective-permute-start(bf16[2,128]{1,0:T(2,128)(2,1)S(1)} %slice.762), channel_id=1, source_target_pairs={{0,1},{1,2},{2,3},{4,5},{5,6},{6,7},{8,9},{9,10},{10,11},{12,13},{... | collective-permute-start | bytes 1544 | tf_op jit(solution)/shard_map/ppermute | solution.py:20
  82.9 4.9 %collective-permute-start.12 = (bf16[4,128]{1,0:T(4,128)(2,1)S(1)}, bf16[4,128]{1,0:T(4,128)(2,1)S(1)}, u32[]{:S(2)}, u32[]{:S(2)}) collective-permute-start(bf16[4,128]{1,0:T(4,128)(2,1)S(1)} %slice.766), channel_id=1, source_target_pairs={{0,1},{1,2},{2,3},{4,5},{5,6},{6,7},{8,9},{9,10},{10,11},{12,13},{... | collective-permute-start | bytes 3080 | tf_op jit(solution)/shard_map/ppermute | solution.py:20
  89.4 4.9 %collective-permute-start.13 = (bf16[8,128]{1,0:T(8,128)(2,1)S(1)}, bf16[8,128]{1,0:T(8,128)(2,1)S(1)}, u32[]{:S(2)}, u32[]{:S(2)}) collective-permute-start(bf16[8,128]{1,0:T(8,128)(2,1)S(1)} %slice.770), channel_id=1, source_target_pairs={{0,1},{1,2},{2,3},{4,5},{5,6},{6,7},{8,9},{9,10},{10,11},{12,13},{... | collective-permute-start | bytes 6152 | tf_op jit(solution)/shard_map/ppermute | solution.py:20
  95.8 4.9 %collective-permute-start.14 = (bf16[16,128]{1,0:T(8,128)(2,1)S(1)}, bf16[16,128]{1,0:T(8,128)(2,1)S(1)}, u32[]{:S(2)}, u32[]{:S(2)}) collective-permute-start(bf16[16,128]{1,0:T(8,128)(2,1)S(1)} %slice.774), channel_id=1, source_target_pairs={{0,1},{1,2},{2,3},{4,5},{5,6},{6,7},{8,9},{9,10},{10,11},{12,13},{... | collective-permute-start | bytes 12296 | tf_op jit(solution)/shard_map/ppermute | solution.py:20
  102.3 5.0 %collective-permute-start.15 = (bf16[32,128]{1,0:T(8,128)(2,1)S(1)}, bf16[32,128]{1,0:T(8,128)(2,1)S(1)}, u32[]{:S(2)}, u32[]{:S(2)}) collective-permute-start(bf16[32,128]{1,0:T(8,128)(2,1)S(1)} %slice.778), channel_id=1, source_target_pairs={{0,1},{1,2},{2,3},{4,5},{5,6},{6,7},{8,9},{9,10},{10,11},{12,13},{... | collective-permute-start | bytes 24584 | tf_op jit(solution)/shard_map/ppermute | solution.py:20
  108.8 5.1 %collective-permute-start.16 = (bf16[64,128]{1,0:T(8,128)(2,1)S(1)}, bf16[64,128]{1,0:T(8,128)(2,1)S(1)}, u32[]{:S(2)}, u32[]{:S(2)}) collective-permute-start(bf16[64,128]{1,0:T(8,128)(2,1)S(1)} %slice.782), channel_id=1, source_target_pairs={{0,1},{1,2},{2,3},{4,5},{5,6},{6,7},{8,9},{9,10},{10,11},{12,13},{... | collective-permute-start | bytes 49160 | tf_op jit(solution)/shard_map/ppermute | solution.py:20
  115.4 5.2 %collective-permute-start.17 = (bf16[128,128]{1,0:T(8,128)(2,1)S(1)}, bf16[128,128]{1,0:T(8,128)(2,1)S(1)}, u32[]{:S(2)}, u32[]{:S(2)}) collective-permute-start(bf16[128,128]{1,0:T(8,128)(2,1)S(1)} %slice.786), channel_id=1, source_target_pairs={{0,1},{1,2},{2,3},{4,5},{5,6},{6,7},{8,9},{9,10},{10,11},{12,13},{... | collective-permute-start | bytes 98312 | tf_op jit(solution)/shard_map/ppermute | solution.py:20
  122.2 5.5 %collective-permute-start.18 = (bf16[256,128]{1,0:T(8,128)(2,1)S(1)}, bf16[256,128]{1,0:T(8,128)(2,1)S(1)}, u32[]{:S(2)}, u32[]{:S(2)}) collective-permute-start(bf16[256,128]{1,0:T(8,128)(2,1)S(1)} %slice.790), channel_id=1, source_target_pairs={{0,1},{1,2},{2,3},{4,5},{5,6},{6,7},{8,9},{9,10},{10,11},{12,13},{... | collective-permute-start | bytes 196616 | tf_op jit(solution)/shard_map/ppermute | solution.py:20
  129.3 6.2 %collective-permute-start.19 = (bf16[512,128]{1,0:T(8,128)(2,1)S(1)}, bf16[512,128]{1,0:T(8,128)(2,1)S(1)}, u32[]{:S(2)}, u32[]{:S(2)}) collective-permute-start(bf16[512,128]{1,0:T(8,128)(2,1)S(1)} %slice.794), channel_id=1, source_target_pairs={{0,1},{1,2},{2,3},{4,5},{5,6},{6,7},{8,9},{9,10},{10,11},{12,13},{... | collective-permute-start | bytes 393224 | tf_op jit(solution)/shard_map/ppermute | solution.py:20
  (6 other events, 11.5 us)
where the time goes:
time: 140 us
  starting transfers between devices  84 us (60%)
  matrix products  31.6 us (23%)
  waiting for transfers between devices  11.8 us (8%)
  other arithmetic  8.37 us (6%)
  local copies, waits for them, and re-layouts  2.25 us (2%)
  between operations  1.82 us (1%)
    ppermute x20, starting transfers between devices, local_stack(): halo_rows = lax.ppermute(hidden[-dilation:], 'sp', perm=shift_perm)  84 us
    ppermute x20, waiting for transfers between devices, local_stack(): halo_rows = lax.ppermute(hidden[-dilation:], 'sp', perm=shift_perm)  11.8 us
    dot_general x20, matrix products, local_stack(): jnp.dot(hidden, w_now[stack_idx, layer_pos], preferred_element_type=jnp.f...  9.3 us
    dot_general x20, matrix products, local_stack(): jnp.dot(shifted, w_past[stack_idx, layer_pos], preferred_element_type=jnp...  8.39 us
    convert_element_type x20, other arithmetic, local_stack(): (jnp.tanh(pre_act[:, :gate_ch]) * jax.nn.sigmoid(pre_act[:, gate_ch:])).a...  8.37 us
    dot_general x20, matrix products, local_stack(): jnp.dot(gated, w_res[stack_idx, layer_pos], preferred_element_type=jnp.fl...  6.33 us
    dot_general x19, matrix products, local_stack(): jnp.dot(gated, w_skip[stack_idx, layer_pos], preferred_element_type=jnp.f...  5.29 us
  transfers between devices with their start and end apart: 20, of which 19 were waited for; matrix products, arithmetic and copies ran while one was open for 5% of the time, Pallas kernels for 0%

commit v1 on v0

v1 whole, which is shorter than its diff:
```python
import functools

import jax
import jax.numpy as jnp
from jax import lax
from jax.experimental import pallas as pl
from jax.experimental.pallas import tpu as pltpu
from jax.sharding import PartitionSpec as P

F32 = jnp.float32
BF16 = jnp.bfloat16
T = 2048
C = 128
EXT = 128
PAD = 64
BASE = PAD + EXT
TILE = 256
HBM = pl.BlockSpec(memory_space=pltpu.HBM)
SENDS = (("x", 128), ("h7", 128), ("h8", 256), ("h9", 512), ("h10", 128), ("h17", 128), ("h18", 256), ("h19", 512))
SLOT = {name: i for i, (name, _) in enumerate(SENDS)}
ROWS = dict(SENDS)
OFFSET = {}
_at = 0
for _name, _rows in SENDS:
    OFFSET[_name] = _at
    _at += _rows
HALO_ROWS = _at


def stack_kernel(x_ref, wp_ref, wn_ref, b_ref, wr_ref, ws_ref, a_out, h_out,
                 hid, pre, skip, keep, send_buf, recv_buf, wp, wn, wr, ws, bias,
                 load_sem, w_sem, send_sem, recv_sem):
    sp = lax.axis_index("sp")
    right = lax.rem(sp + 1, 4)
    left = lax.rem(sp + 3, 4)
    first = sp == 0

    barrier = pltpu.get_barrier_semaphore()
    pl.semaphore_signal(barrier, inc=1, device_id={"sp": left}, device_id_type=pl.DeviceIdType.MESH)

    def remote(name, src):
        rows = ROWS[name]
        return pltpu.make_async_remote_copy(
            src_ref=src,
            dst_ref=recv_buf.at[pl.ds(OFFSET[name], rows)],
            send_sem=send_sem.at[SLOT[name]],
            recv_sem=recv_sem.at[SLOT[name]],
            device_id={"sp": right},
            device_id_type=pl.DeviceIdType.MESH,
        )

    def send_of(name):
        if name == "x":
            return remote(name, x_ref.at[pl.ds(T - EXT, EXT)])
        return remote(name, send_buf.at[pl.ds(OFFSET[name], ROWS[name])])

    load_x = pltpu.make_async_copy(x_ref, hid.at[pl.ds(BASE, T)], load_sem.at[0])
    load_b = pltpu.make_async_copy(b_ref, bias, load_sem.at[1])
    load_pre = pltpu.make_async_copy(x_ref.at[pl.ds(0, 128)], pre.at[pl.ds(BASE, 128)], load_sem.at[2])
    groups = ((0, 0, 1), (0, 1, 9), (1, 0, 10))
    w_loads = []
    for g, (s, k0, n) in enumerate(groups):
        w_loads.append([
            pltpu.make_async_copy(src.at[s, pl.ds(k0, n)], dst.at[s, pl.ds(k0, n)], w_sem.at[g, i])
            for i, (src, dst) in enumerate(((wp_ref, wp), (wn_ref, wn), (wr_ref, wr), (ws_ref, ws)))
        ])
    load_x.start()
    load_b.start()
    for copies in w_loads:
        for copy in copies:
            copy.start()
    load_pre.start()
    hid[pl.ds(0, BASE), :] = jnp.zeros((BASE, C), BF16)
    pre[pl.ds(0, PAD), :] = jnp.zeros((PAD, C), BF16)

    pl.semaphore_wait(barrier, 1)
    send_of("x").start()

    def halo(name, lo, n):
        rows = recv_buf[pl.ds(OFFSET[name] + lo, n), :]
        return jnp.where(first, jnp.zeros_like(rows), rows)

    def tile(l, r0, r1, buf, past_of, skip_from, skip_init=False, zero_to=None, tail=None):
        s, k = divmod(l, 10)
        n = r1 - r0
        now = buf[pl.ds(BASE + r0, n), :]
        past = past_of(r0, n)
        w = jnp.concatenate([wp[s, k], wn[s, k]], axis=0)
        z = jnp.dot(jnp.concatenate([past, now], axis=1), w, preferred_element_type=F32)
        z = z + bias[s, pl.ds(k, 1), :]
        gate = 0.5 * jnp.tanh(0.5 * z[:, C:]) + 0.5
        g = (jnp.tanh(z[:, :C]) * gate).astype(BF16)
        out = jnp.dot(g, jnp.concatenate([wr[s, k], ws[s, k]], axis=1), preferred_element_type=F32)
        new = (now.astype(F32) + out[:, :C]).astype(BF16)
        if zero_to is not None and r0 < zero_to:
            m = zero_to - r0
            head = jnp.where(first, jnp.zeros((m, C), BF16), new[:m])
            new = head if m == n else jnp.concatenate([head, new[m:]], axis=0)
        if l == 19:
            h_out[pl.ds(r0, n), :] = new
        else:
            buf[pl.ds(BASE + r0, n), :] = new
        if tail is not None and r1 > T - ROWS[tail]:
            cut = max(T - ROWS[tail] - r0, 0)
            send_buf[pl.ds(OFFSET[tail] + r0 + cut - (T - ROWS[tail]), n - cut), :] = new[cut:]
        lo = max(r0, skip_from)
        if lo < r1:
            add = out[lo - r0:, C:]
            rows = pl.ds(lo, r1 - lo)
            total = add if skip_init else skip[rows, :] + add
            if l == 19:
                a_out[rows, :] = jnp.maximum(total, 0.0).astype(BF16)
            else:
                skip[rows, :] = total

    def tiles(lo, hi, step=TILE):
        cuts = []
        r1 = hi
        while r1 > lo:
            r0 = max(lo, -(-r1 // step) * step - step)
            cuts.append((r0, r1))
            r1 = r0
        return cuts

    def past_in(buf, d):
        return lambda r0, n: buf[pl.ds(BASE + r0 - d, n), :]

    def past_halo(name, d):
        def get(r0, n):
            if r0 >= d:
                return hid[pl.ds(BASE + r0 - d, n), :]
            m = min(n, d - r0)
            part = halo(name, r0, m)
            if m == n:
                return part
            return jnp.concatenate([part, hid[pl.ds(BASE, n - m), :]], axis=0)
        return get

    def layer(l, lo, hi, skip_from, tail=None, halo_name=None, zero_to=None, buf=None):
        d = 2 ** (l % 10)
        buf = hid if buf is None else buf
        past = past_halo(halo_name, d) if halo_name else past_in(buf, d)
        cuts = tiles(lo, hi)
        for i, (r0, r1) in enumerate(cuts):
            due = list(pending)
            tile(l, r0, r1, buf, past, skip_from, skip_init=(l == 0), zero_to=zero_to, tail=tail)
            for name in due:
                send_of(name).start()
                pending.remove(name)
            if tail is not None and r0 <= T - ROWS[tail] < r1:
                pending.append(tail)

    pending = []

    def flush():
        for name in pending:
            send_of(name).start()
        pending.clear()

    load_x.wait()
    load_b.wait()
    for copy in w_loads[0]:
        copy.wait()
    layer(0, 0, T, 128)
    for copy in w_loads[1]:
        copy.wait()
    for l in range(1, 7):
        layer(l, 0, T, 128, tail="h7" if l == 6 else None)
    layer(7, 256, T, 128, tail="h8")
    layer(8, 512, T, 128, tail="h9")
    layer(9, 1024, T, 128, tail="h10")
    for copy in w_loads[2]:
        copy.wait()
    keep[...] = hid[pl.ds(BASE + 1024, 128), :]

    send_of("x").wait_recv()
    load_pre.wait()
    pre[pl.ds(PAD, EXT), :] = halo("x", 0, EXT)
    for k in range(7):
        layer(10 + k, 1024, T, 1152, tail="h17" if k == 6 else None)
        layer(k, -EXT, 128, 0, zero_to=0, buf=pre)
    layer(17, 1280, T, 0, tail="h18")
    layer(18, 1536, T, 0, tail="h19")

    hid[pl.ds(BASE, 128), :] = pre[pl.ds(BASE, 128), :]
    hid[pl.ds(BASE + 1024, 128), :] = keep[...]
    for l, hi in ((7, 256), (8, 512), (9, 1024)):
        send_of(f"h{l}").wait_recv()
        layer(l, 0, hi, 0, halo_name=f"h{l}")

    send_of("h10").wait_recv()
    hid[pl.ds(PAD, EXT), :] = halo("h10", 0, EXT)
    for l in range(10, 17):
        layer(l, -EXT, 1152, 0, zero_to=0)
    for l, hi in ((17, 1280), (18, 1536), (19, T)):
        send_of(f"h{l}").wait_recv()
        layer(l, 0, hi, 0, halo_name=f"h{l}")
    flush()
    for name, _ in SENDS:
        send_of(name).wait_send()


def head_kernel(a_ref, h_ref, w1_ref, c1_ref, w2_ref, c2_ref, y_ref, h_out):
    m = jnp.dot(a_ref[...], w1_ref[...], preferred_element_type=F32) + c1_ref[...]
    m = jnp.maximum(m, 0.0).astype(BF16)
    y_ref[...] = jnp.dot(m, w2_ref[...], preferred_element_type=F32) + c2_ref[...]
    h_out[...] = h_ref[...]


def solution(mesh):
    row_spec = P(("ens", "sp"), None)

    def local_stack(x_seq, w_past, w_now, b_conv, w_res, w_skip, w_out1, b_out1, w_out2, b_out2):
        vmem = pl.BlockSpec(memory_space=pltpu.VMEM)
        a, h = pl.pallas_call(
            stack_kernel,
            out_shape=(jax.ShapeDtypeStruct((T, C), BF16), jax.ShapeDtypeStruct((T, C), BF16)),
            in_specs=[HBM] * 6,
            out_specs=(vmem, vmem),
            scratch_shapes=[
                pltpu.VMEM((BASE + T, C), BF16),
                pltpu.VMEM((BASE + 128, C), BF16),
                pltpu.VMEM((T, C), F32),
                pltpu.VMEM((128, C), BF16),
                pltpu.VMEM((HALO_ROWS, C), BF16),
                pltpu.VMEM((HALO_ROWS, C), BF16),
                pltpu.VMEM((2, 10, C, 2 * C), BF16),
                pltpu.VMEM((2, 10, C, 2 * C), BF16),
                pltpu.VMEM((2, 10, C, C), BF16),
                pltpu.VMEM((2, 10, C, C), BF16),
                pltpu.VMEM((2, 10, 2 * C), F32),
                pltpu.SemaphoreType.DMA((3,)),
                pltpu.SemaphoreType.DMA((3, 4)),
                pltpu.SemaphoreType.DMA((len(SENDS),)),
                pltpu.SemaphoreType.DMA((len(SENDS),)),
            ],
            compiler_params=pltpu.CompilerParams(
                collective_id=0, has_side_effects=True, vmem_limit_bytes=65_600_000),
            name="stack",
        )(x_seq, w_past, w_now, b_conv, w_res, w_skip)
        step = 512
        rows = lambda width: pl.BlockSpec((step, width), lambda i: (i, 0))
        whole = lambda *shape: pl.BlockSpec(shape, lambda i: (0,) * len(shape))
        return pl.pallas_call(
            head_kernel,
            grid=(T // step,),
            out_shape=(jax.ShapeDtypeStruct((T, 2 * C), F32), jax.ShapeDtypeStruct((T, C), BF16)),
            in_specs=[rows(C), rows(C), whole(C, C), whole(1, C), whole(C, 2 * C), whole(1, 2 * C)],
            out_specs=(rows(2 * C), rows(C)),
            compiler_params=pltpu.CompilerParams(vmem_limit_bytes=16 * 1024 * 1024),
            name="head",
        )(a, h, w_out1, b_out1.reshape(1, C), w_out2, b_out2.reshape(1, 2 * C))

    return jax.shard_map(
        local_stack,
        mesh=mesh,
        in_specs=(row_spec, P(), P(), P(), P(), P(), P(), P(), P(), P()),
        out_specs=(row_spec, row_spec),
        check_vma=False,
    )
```

time: 140 us -> 28.7 us (0.20)
  starting transfers between devices: 84 us -> 0 us
  matrix products: 31.6 us -> 0 us
  Pallas kernels: 0 us -> 24.3 us
  waiting for transfers between devices: 11.8 us -> 0 us
  other arithmetic: 8.37 us -> 0 us
    ppermute x20 -> x0, starting transfers between devices: 84 us -> none  [local_stack(): halo_rows = lax.ppermute(hidden[-dilation:], 'sp', perm=shift_perm)]
    dot_general x81 -> x0, matrix products: 31.6 us -> none  [the longest x20 9.3 us: local_stack(): jnp.dot(hidden, w_now[stack_idx, layer_pos], preferred_element_type=jnp.f...]
    pallas_call x0 -> x2, Pallas kernels: none -> 24.3 us  [the longest x1 21.6 us: local_stack(): pl.pallas_call(stack_kernel, out_shape=(jax.ShapeDtypeStruct((T, C), BF16...]
    ppermute x20 -> x0, waiting for transfers between devices: 11.8 us -> none  [local_stack(): halo_rows = lax.ppermute(hidden[-dilation:], 'sp', perm=shift_perm)]
    convert_element_type x20 -> x0, other arithmetic: 8.37 us -> none  [local_stack(): (jnp.tanh(pre_act[:, :gate_ch]) * jax.nn.sigmoid(pre_act[:, gate_ch:])).a...]
    unnamed x20 -> x13, local copies, waits for them, and re-layouts: 0.84 us -> 3.44 us
    slice x36 -> x0, local copies, waits for them, and re-layouts: 1.41 us -> none  [the longest x20 0.92 us: local_stack(): halo_rows = lax.ppermute(hidden[-dilation:], 'sp', perm=shift_perm)]
  transfers between devices with their start and end apart: 20 -> 0, of which waited for: 19 -> 0; matrix products, arithmetic and copies ran while one was open for 5% -> 0% of each run, Pallas kernels for 0% -> 0%
where the time goes in v1:
time: 28.7 us; the launch traced here: 28.5 us
  Pallas kernels  24.3 us (85%)
  local copies, waits for them, and re-layouts  3.44 us (12%)
  between operations  0.68 us (2%)
    pallas_call x1, Pallas kernels, local_stack(): pl.pallas_call(stack_kernel, out_shape=(jax.ShapeDtypeStruct((T, C), BF16...  21.6 us
    unnamed x13, local copies, waits for them, and re-layouts  3.44 us
    pallas_call x1, Pallas kernels, local_stack(): pl.pallas_call(head_kernel, grid=(T // step,), out_shape=(jax.ShapeDtypeS...  2.73 us

profile of v1, /device:TPU:1, one launch (start us, length us, event | category | flops | bytes accessed | tf_op | source)
XLA Modules:
  0.0 28.5 jit_solution(8504118570348698089)
XLA Ops:
  0.6 1.3 %copy.12.b_ref = f32[2,10,256]{2,1,0:T(8,128)} copy(f32[2,10,256]{2,0,1:T(2,128)} %param.13) | data formatting | bytes 40960 | tf_op args[3]
  2.0 0.0 copy-start.2
  2.0 0.0 copy-start.3
  2.0 0.0 copy-start.4
  2.0 0.0 copy-start.5
  2.0 21.6 %stack.1 = (bf16[2048,128]{1,0:T(8,128)(2,1)}, bf16[2048,128]{1,0:T(8,128)(2,1)}) custom-call(bf16[2048,128]{1,0:T(8,128)(2,1)} %x_ref.1, bf16[2,10,128,256]{3,2,1,0:T(8,128)(2,1)} %wp_ref.1, bf16[2,10,128,256]{3,2,1,0:T(8,128)(2,1)} %wn_ref.1, f32[2,10,256]{2,1,0:T(8,128)} %copy.12.b_ref, bf16[2,10,128,128]{3,2,1,0:T(8,128)(2,1)} %wr_ref.1, ...), custom_call_target="tpu_custom_call" | custom-call | tf_op jit(solution)/shard_map/stack/pallas_call | solution.py:215
  23.6 0.0 copy-done.2
  23.6 0.0 copy-done.3
  23.6 0.0 copy-done.4
  23.6 0.0 copy-done.5
  23.6 0.0 copy-start
  23.6 1.0 %copy-done = bf16[2048,128]{1,0:T(8,128)(2,1)S(1)} copy-done((bf16[2048,128]{1,0:T(8,128)(2,1)S(1)}, bf16[2048,128]{1,0:T(8,128)(2,1)}, u32[]{:S(2)}) %copy-start) | copy-done | bytes 524312
  24.7 0.0 copy-start.1
  24.7 1.0 %copy-done.1 = bf16[2048,128]{1,0:T(8,128)(2,1)S(1)} copy-done((bf16[2048,128]{1,0:T(8,128)(2,1)S(1)}, bf16[2048,128]{1,0:T(8,128)(2,1)}, u32[]{:S(2)}) %copy-start.1) | copy-done | bytes 524312
  25.7 2.7 %head.1 = (f32[2048,256]{1,0:T(8,128)}, bf16[2048,128]{1,0:T(8,128)(2,1)}) custom-call(bf16[2048,128]{1,0:T(8,128)(2,1)S(1)} %copy-done, bf16[2048,128]{1,0:T(8,128)(2,1)S(1)} %copy-done.1, bf16[128,128]{1,0:T(8,128)(2,1)S(1)} %copy-done.3, f32[1,128]{1,0:T(1,128)S(1)} %bitcast.3, bf16[128,256]{1,0:T(8,128)(2,1)S(1)} %copy-done.2, f32[1,256]{1,0:T(1,128)S(1)} %bitcast.2), custom_call_target="tpu_custom_call" | custom-call | tf_op jit(solution)/shard_map/head/pallas_call | solution.py:244
Async XLA Ops:
  2.0 21.6 %copy-start.2 = (bf16[128,256]{1,0:T(8,128)(2,1)S(1)}, bf16[128,256]{1,0:T(8,128)(2,1)}, u32[]{:S(2)}) copy-start(bf16[128,256]{1,0:T(8,128)(2,1)} %w2_ref.1) | copy-start | bytes 196612
  2.0 21.6 %copy-start.3 = (bf16[128,128]{1,0:T(8,128)(2,1)S(1)}, bf16[128,128]{1,0:T(8,128)(2,1)}, u32[]{:S(2)}) copy-start(bf16[128,128]{1,0:T(8,128)(2,1)} %w1_ref.1) | copy-start | bytes 98308
  2.0 21.6 %copy-start.4 = (f32[256]{0:T(256)S(1)}, f32[256]{0:T(256)}, u32[]{:S(2)}) copy-start(f32[256]{0:T(256)} %param.19) | copy-start | bytes 3076
  2.0 21.6 %copy-start.5 = (f32[128]{0:T(128)S(1)}, f32[128]{0:T(128)}, u32[]{:S(2)}) copy-start(f32[128]{0:T(128)} %param.17) | copy-start | bytes 1540
  23.6 1.0 %copy-start = (bf16[2048,128]{1,0:T(8,128)(2,1)S(1)}, bf16[2048,128]{1,0:T(8,128)(2,1)}, u32[]{:S(2)}) copy-start(bf16[2048,128]{1,0:T(8,128)(2,1)} %get-tuple-element.4.a_ref) | copy-start | bytes 1572868
  24.7 1.0 %copy-start.1 = (bf16[2048,128]{1,0:T(8,128)(2,1)S(1)}, bf16[2048,128]{1,0:T(8,128)(2,1)}, u32[]{:S(2)}) copy-start(bf16[2048,128]{1,0:T(8,128)(2,1)} %get-tuple-element.5.h_ref) | copy-start | bytes 1572868
